TPU v7x, 128 devices: a whole 4x4x4 slice. The times are simulated.
128 devices in a mesh: owner: 4 (over x_lo, core), rows: 32 (over z, y, x_hi).
Axes of the slice: x: 4 (x_hi: 2, x_lo: 2; x = x_hi * 2 + x_lo), y: 4, z: 4, core: 2. Of those that a mesh axis runs over, the one named last changes fastest.
Arguments:
- master_down: float32 [8, 14336, 4096], P('owner', None, 'rows'), may hold values from -0.046875 to 0.046875
- router_weight: float32 [4096, 8], P('rows', 'owner'), may hold values from -0.09375 to 0.09375
- router_gain: float32 [4096], P('rows'), may hold values from 0.25 to 1.75
Outputs:
- final_down: bfloat16 [8, 4096, 14336], P('owner', None, 'rows')
- serve_router: bfloat16 [4096, 8], replicated
All inputs are finite; a program needn't handle non-finite values.
Results may differ from a plain program's by a relative error of at most 0.001.
Values may be sent and summed in bfloat16 or wider, within the bound.
A program may use at most 128 MiB of HBM per device.

v0:
```python
import jax
import jax.numpy as jnp
from jax import lax
from jax.sharding import Mesh
from jax.sharding import PartitionSpec as P

OWNER = ("owner_0", "owner_1")


def in_blocks(value, dim, size):
    lengths = value.shape
    blocks = value.reshape(*lengths[:dim], size, lengths[dim] // size, *lengths[dim + 1 :])
    return jnp.moveaxis(blocks, dim, 0)


def edges_of(length, count):
    lap = length // count
    if lap >= 8:
        lap -= lap % 8
    return [lap * k for k in range(1, count)]


def laid_out(blocks, dim):
    lengths = list(blocks.shape[1:])
    lengths[dim] *= blocks.shape[0]
    return jnp.moveaxis(blocks, 0, dim).reshape(lengths)


def cut_exchange(value, axis, pieces, split_dim, concat_dim):
    blocks = in_blocks(value, split_dim, lax.axis_size(axis))
    split_at = max(range(1, max(2, blocks.ndim - 1)), key=lambda d: blocks.shape[d])
    gathered = []
    for slab in jnp.split(blocks, edges_of(blocks.shape[split_at], pieces), axis=split_at):
        if slab.size:
            gathered.append(lax.all_to_all(slab, axis, split_axis=0, concat_axis=0, tiled=True))
    return laid_out(jnp.concatenate(gathered, axis=split_at), concat_dim)


def sent_to_all(value, axis):
    size = lax.axis_size(axis)
    return lax.all_to_all(
        jnp.broadcast_to(value[None], (size, *value.shape)), axis, 0, 0, tiled=True
    )


def gather_directly(value, axis, dim):
    return laid_out(sent_to_all(value, axis), dim)


def all_blocks(value, axes, sequence):
    blocks = value
    for k in sequence:
        blocks = lax.all_gather(blocks, axes[k])
    done = sequence[::-1]
    back = [done.index(k) for k in range(len(axes))]
    blocks = blocks.transpose(*back, *range(len(axes), blocks.ndim))
    return blocks.reshape(-1, *value.shape)


def whole_of(value, axes, sequence, dim):
    return laid_out(all_blocks(value, axes, sequence), dim)


def shards(master_down, router_weight, router_gain):
    narrow_down = master_down.astype(jnp.bfloat16)
    final_down = cut_exchange(narrow_down, "rows", 2, 1, 2)
    final_down = jnp.transpose(final_down, (0, 2, 1))
    part_router = (router_weight * router_gain[:, None]).astype(jnp.bfloat16)
    row_router = gather_directly(part_router, "rows", 0)
    serve_router = whole_of(row_router, OWNER, (0, 1), 1)
    return (final_down, serve_router)


def solution(mesh):
    finer = Mesh(mesh.devices.reshape(2, 2, mesh.shape["rows"]), ("owner_0", "owner_1", "rows"))
    return jax.shard_map(
        shards,
        mesh=finer,
        in_specs=(P(OWNER, None, "rows"), P("rows", OWNER), P("rows")),
        out_specs=(P(OWNER, None, "rows"), P()),
        check_vma=False,
    )
```

profile of v0, /device:TPU:0, one launch (start us, length us, event | category | flops | bytes accessed | tf_op | source)
XLA Modules:
  0.0 141.8 jit_solution(14652387285458491345)
XLA Ops:
  0.6 0.7 multiply_convert_fusion
  1.3 0.6 broadcast_in_dim.2
  1.9 10.9 %all-to-all-start.2 = ((bf16[32,128,2]{1,2,0:T(2,128)(2,1)}), bf16[32,128,2]{1,2,0:T(2,128)(2,1)S(1)}, u32[]{:S(2)}, u32[]{:S(2)}) async-start(bf16[32,128,2]{1,2,0:T(2,128)(2,1)} %broadcast_in_dim.2), calls=%async_computation.2 | async-start | bytes 32768 | tf_op jit(solution)/shard_map/all_to_all | solution.py:41
  12.8 5.8 %convert_element_type.6 = bf16[2,14336,128]{2,1,0:T(8,128)(2,1)S(1)} convert(f32[2,14336,128]{2,1,0:T(8,128)} %param.3) | non-fusion elementwise | flops 3670016 | bytes 22020096 | tf_op jit(solution)/shard_map/convert_element_type | solution.py:65
  18.7 2.4 %fusion = (bf16[32,2,224,128]{3,2,0,1:T(8,128)(2,1)S(1)}, bf16[32,2,224,128]{3,2,0,1:T(8,128)(2,1)}) fusion(bf16[32,2,448,128]{3,2,0,1:T(8,128)(2,1)S(1)} %bitcast.20), kind=kLoop, calls=%fused_computation.3 | loop fusion | bytes 14680064 | tf_op jit(solution)/shard_map/split | solution.py:33
  21.1 2.3 %copy.11 = bf16[32,2,224,128]{3,2,1,0:T(8,128)(2,1)} copy(bf16[32,2,224,128]{3,2,0,1:T(8,128)(2,1)S(1)} %get-tuple-element.2) | data formatting | bytes 7340032 | tf_op jit(solution)/shard_map/split | solution.py:33
  23.4 0.0 all-to-all-done.2
  23.4 9.9 %all-to-all-start = ((bf16[32,2,224,128]{3,2,1,0:T(8,128)(2,1)}), bf16[32,2,224,128]{3,2,1,0:T(8,128)(2,1)}, u32[]{:S(2)}, u32[]{:S(2)}) async-start(bf16[32,2,224,128]{3,2,1,0:T(8,128)(2,1)} %copy.11), calls=%async_computation | async-start | bytes 7340032 | tf_op jit(solution)/shard_map/all_to_all | solution.py:35
  33.3 4.5 %copy.12 = bf16[32,2,224,128]{3,2,1,0:T(8,128)(2,1)} copy(bf16[32,2,224,128]{3,2,0,1:T(8,128)(2,1)} %get-tuple-element.3) | data formatting | bytes 7340032 | tf_op jit(solution)/shard_map/split | solution.py:33
  37.8 42.5 %all-to-all-done = bf16[32,2,224,128]{3,2,1,0:T(8,128)(2,1)} async-done(((bf16[32,2,224,128]{3,2,1,0:T(8,128)(2,1)}), bf16[32,2,224,128]{3,2,1,0:T(8,128)(2,1)}, u32[]{:S(2)}, u32[]{:S(2)}) %all-to-all-start) | async-done | bytes 3670048 | tf_op jit(solution)/shard_map/all_to_all | solution.py:35
  80.3 8.1 %all-to-all-start.1 = ((bf16[32,2,224,128]{3,2,1,0:T(8,128)(2,1)}), bf16[32,2,224,128]{3,2,1,0:T(8,128)(2,1)}, u32[]{:S(2)}, u32[]{:S(2)}) async-start(bf16[32,2,224,128]{3,2,1,0:T(8,128)(2,1)} %copy.12), calls=%async_computation.1 | async-start | bytes 7340032 | tf_op jit(solution)/shard_map/all_to_all | solution.py:35
  88.4 41.5 %all_gather.9 = bf16[2,4096,2]{1,2,0:T(2,128)(2,1)S(1)} all-gather(bf16[1,4096,2]{1,2,0:T(2,128)(2,1)S(1)} %bitcast.23), channel_id=1, replica_groups=mesh['owner_0'=2,'owner_1'=2,'rows'=32] {'owner_0'}, dimensions={0}, use_global_device_ids=true | all-gather | bytes 49152 | tf_op jit(solution)/shard_map/all_gather | solution.py:53
  129.9 1.8 %all-gather = bf16[4,4096,2]{1,2,0:T(2,128)(2,1)S(1)} all-gather(bf16[2,4096,2]{1,2,0:T(2,128)(2,1)S(1)} %all_gather.9), channel_id=2, replica_groups=mesh['owner_0'=2,'owner_1'=2,'rows'=32] {'owner_1'}, dimensions={0}, use_global_device_ids=true | all-gather | bytes 98304 | tf_op jit(solution)/shard_map/all_gather | solution.py:53
  131.8 0.7 reshape.21
  132.5 2.7 %all-to-all-done.1 = bf16[32,2,224,128]{3,2,1,0:T(8,128)(2,1)} async-done(((bf16[32,2,224,128]{3,2,1,0:T(8,128)(2,1)}), bf16[32,2,224,128]{3,2,1,0:T(8,128)(2,1)}, u32[]{:S(2)}, u32[]{:S(2)}) %all-to-all-start.1) | async-done | bytes 3670048 | tf_op jit(solution)/shard_map/all_to_all | solution.py:35
  135.2 6.7 %bitcast_bitcast_fusion = bf16[2,4096,448]{1,2,0:T(8,128)(2,1)} fusion(bf16[32,2,224,128]{3,2,1,0:T(8,128)(2,1)} %all-to-all-done.1, bf16[32,2,224,128]{3,2,1,0:T(8,128)(2,1)} %all-to-all-done), kind=kLoop, calls=%fused_computation | loop fusion | flops 14680064 | bytes 14680064 | tf_op jit(solution)/shard_map/transpose | solution.py:67
  (1 shorter events, 0.0 us)
Async XLA Ops:
  1.9 21.5 %all-to-all-start.2 = ((bf16[32,128,2]{1,2,0:T(2,128)(2,1)}), bf16[32,128,2]{1,2,0:T(2,128)(2,1)S(1)}, u32[]{:S(2)}, u32[]{:S(2)}) async-start(bf16[32,128,2]{1,2,0:T(2,128)(2,1)} %broadcast_in_dim.2), calls=%async_computation.2 | async-start | bytes 32768 | tf_op jit(solution)/shard_map/all_to_all | solution.py:41
  23.4 56.9 %all-to-all-start = ((bf16[32,2,224,128]{3,2,1,0:T(8,128)(2,1)}), bf16[32,2,224,128]{3,2,1,0:T(8,128)(2,1)}, u32[]{:S(2)}, u32[]{:S(2)}) async-start(bf16[32,2,224,128]{3,2,1,0:T(8,128)(2,1)} %copy.11), calls=%async_computation | async-start | bytes 7340032 | tf_op jit(solution)/shard_map/all_to_all | solution.py:35
  80.3 54.9 %all-to-all-start.1 = ((bf16[32,2,224,128]{3,2,1,0:T(8,128)(2,1)}), bf16[32,2,224,128]{3,2,1,0:T(8,128)(2,1)}, u32[]{:S(2)}, u32[]{:S(2)}) async-start(bf16[32,2,224,128]{3,2,1,0:T(8,128)(2,1)} %copy.12), calls=%async_computation.1 | async-start | bytes 7340032 | tf_op jit(solution)/shard_map/all_to_all | solution.py:35
where the time goes:
time: 144 us; the launch traced here: 142 us
  waiting for transfers between devices  45.2 us (31%)
  blocking collectives  43.4 us (30%)
  starting transfers between devices  28.9 us (20%)
  other arithmetic  13.2 us (9%)
  local copies, waits for them, and re-layouts  10.5 us (7%)
    all_to_all x2, waiting for transfers between devices, cut_exchange(): lax.all_to_all(slab, axis, split_axis=0, concat_axis=0, tiled=True)  45.2 us
    all_gather x2, blocking collectives, all_blocks(): blocks = lax.all_gather(blocks, axes[k])  43.4 us
    all_to_all x2, starting transfers between devices, cut_exchange(): lax.all_to_all(slab, axis, split_axis=0, concat_axis=0, tiled=True)  18 us
    all_to_all x1, starting transfers between devices, sent_to_all(): lax.all_to_all(jnp.broadcast_to(value[None], (size, *value.shape)), axis,...  10.9 us
    split x3, local copies, waits for them, and re-layouts, cut_exchange(): jnp.split(blocks, edges_of(blocks.shape[split_at], pieces), axis=split_at)  9.21 us
    transpose x1, other arithmetic, shards(): final_down = jnp.transpose(final_down, (0, 2, 1))  6.65 us
    convert_element_type x1, other arithmetic, shards(): narrow_down = master_down.astype(jnp.bfloat16)  5.81 us
  transfers between devices with their start and end apart: 3, of which 2 were waited for; matrix products, arithmetic and copies ran while one was open for 11% of the time, Pallas kernels for 0%

commit v1 on v0

v1 whole, which is shorter than its diff:
```python
import functools
import itertools

import jax
import jax.numpy as jnp
from jax import lax
from jax.experimental import pallas as pl
from jax.experimental.pallas import tpu as pltpu
from jax.sharding import PartitionSpec as P

MESH = pl.DeviceIdType.MESH
SIZES = (4, 4, 2)
ORDERS = ((0, 1, 2), (1, 2, 0), (2, 0, 1))
OWNERS = 4


def cuts_of(length, count, step):
    tiles = length // step
    edges = [tiles * k // count * step for k in range(count)] + [length]
    return [(a, b - a) for a, b in zip(edges, edges[1:])]


def flat(delta):
    index = 0
    for d, size in zip(delta, SIZES):
        index = index * size + d
    return index


DELTAS = sorted(
    itertools.product(*(range(s) for s in SIZES)),
    key=lambda d: (sum(k == 0 for k in d), d[0] == 2, d[1] == 2, d),
)
OTHERS = [d for d in DELTAS if any(d)]


def travelled(color, phase, delta):
    return [q for q in range(phase) if delta[ORDERS[color][q]]]


def is_final(color, phase, delta):
    return not any(delta[ORDERS[color][q]] for q in range(phase + 1, 3))


def kernel(rows_axis, owner_axis, cuts, x_ref, w_ref, g_ref, out_ref, router_ref, loaded, held, first, second,
           parts, grid, load_sem, send_sem, recv_sem, part_send, part_recv, grid_send, grid_recv):
    me = lax.axis_index(rows_axis)
    own = lax.axis_index(owner_axis)
    place = (me // 8, (me // 2) % 4, me % 2)
    depth = held.shape[2]
    width = held.shape[3]
    relays = (first, second)

    def index_at(coords):
        return (coords[0] * SIZES[1] + coords[1]) * SIZES[2] + coords[2]

    def moved(delta, sign=1):
        return index_at([lax.rem(p + sign * d + s, s) if d else p for p, d, s in zip(place, delta, SIZES)])

    def along(dim, step):
        return moved([step if k == dim else 0 for k in range(3)])

    peers = {(d, k): along(d, k) for d in range(3) for k in range(1, SIZES[d])}
    mates = [lax.rem(own + k, OWNERS) for k in range(OWNERS)]

    barrier = pltpu.get_barrier_semaphore()
    for peer in peers.values():
        pl.semaphore_signal(barrier, inc=1, device_id=(own, peer), device_id_type=MESH)
    for k in range(1, OWNERS):
        pl.semaphore_signal(barrier, inc=1, device_id=(mates[k], me), device_id_type=MESH)

    def load(delta):
        i = flat(delta)
        start = pl.multiple_of(moved(delta) * depth, 8)
        return pltpu.make_async_copy(x_ref.at[:, pl.ds(start, depth), :], loaded.at[i], load_sem.at[i])

    for delta in DELTAS:
        load(delta).start()

    def copy(color, phase, delta):
        i = flat(delta)
        start, size = cuts[color]
        rows = pl.ds(start, size)
        before = travelled(color, phase, delta)
        source = (relays[before[-1]] if before else held).at[i, :, rows, :]
        dim = ORDERS[color][phase]
        if is_final(color, phase, delta):
            gone = [0, 0, 0]
            for q in before:
                gone[ORDERS[color][q]] = delta[ORDERS[color][q]]
            column = pl.multiple_of(moved(gone, -1) * width, 128)
            target = out_ref.at[:, rows, pl.ds(column, width)]
        else:
            target = relays[phase].at[i, :, rows, :]
        return pltpu.make_async_remote_copy(
            src_ref=source, dst_ref=target, send_sem=send_sem.at[color, phase, i], recv_sem=recv_sem.at[color, phase, i],
            device_id=(own, peers[dim, delta[dim]]), device_id_type=MESH)

    def goes(color, phase, delta):
        return delta[ORDERS[color][phase]] != 0

    scaled = (w_ref[...] * g_ref[...]).astype(jnp.bfloat16).astype(jnp.float32)
    line = lax.broadcasted_iota(jnp.int32, (8, width), 0)
    pair = jnp.where(line % 2 == 0, jnp.broadcast_to(scaled[0:1, :], (8, width)), jnp.broadcast_to(scaled[1:2, :], (8, width)))
    parts[0] = pair.astype(jnp.bfloat16)

    def part_copy(k):
        return pltpu.make_async_remote_copy(
            src_ref=parts.at[0], dst_ref=parts.at[k], send_sem=part_send.at[k], recv_sem=part_recv.at[k],
            device_id=(mates[k], me), device_id_type=MESH)

    def grid_copies(dim):
        if dim == 0:
            block = grid.at[place[0], place[1], place[2]]
        elif dim == 1:
            block = grid.at[:, place[1], place[2]]
        else:
            block = grid.at[:, :, place[2]]
        return [
            pltpu.make_async_remote_copy(
                src_ref=block, dst_ref=block, send_sem=grid_send.at[dim, k], recv_sem=grid_recv.at[dim, k],
                device_id=(own, peers[dim, k]), device_id_type=MESH)
            for k in range(1, SIZES[dim])
        ]

    pl.semaphore_wait(barrier, len(peers) + OWNERS - 1)

    waiting = None
    for delta in DELTAS:
        load(delta).wait()
        if any(delta):
            held[flat(delta)] = loaded[flat(delta)].astype(jnp.bfloat16)
        else:
            out_ref[:, :, pl.ds(pl.multiple_of(me * width, 128), width)] = loaded[flat(delta)].astype(jnp.bfloat16)
        if waiting is not None:
            for color in range(3):
                if goes(color, 0, waiting):
                    copy(color, 0, waiting).start()
        waiting = delta if any(delta) else None
    for k in range(1, OWNERS):
        part_copy(k).start()

    for delta in OTHERS:
        for color in range(3):
            if goes(color, 1, delta) and not travelled(color, 1, delta):
                copy(color, 1, delta).start()

    for k in range(1, OWNERS):
        part_copy(k).wait()
    tile = parts[0].astype(jnp.float32)
    for k in range(1, OWNERS):
        theirs = lax.rem(own - k + OWNERS, OWNERS)
        tile = jnp.where(line // 2 == theirs, parts[k].astype(jnp.float32), tile)
    grid[place[0], place[1], place[2]] = tile.astype(jnp.bfloat16)

    count = 0
    for delta in OTHERS:
        for color in range(3):
            if goes(color, 0, delta) and not is_final(color, 0, delta):
                copy(color, 0, delta).wait_recv()
                if goes(color, 1, delta):
                    copy(color, 1, delta).start()
                count += 1
                if count == 4:
                    for c in grid_copies(0):
                        c.start()
                if count == 24:
                    for c in grid_copies(0):
                        c.wait()
                    for c in grid_copies(1):
                        c.start()
                if count == 48:
                    for c in grid_copies(1):
                        c.wait()
                    for c in grid_copies(2):
                        c.start()

    for late in ([], [0]):
        for delta in OTHERS:
            for color in range(3):
                if goes(color, 2, delta) and travelled(color, 2, delta) == late:
                    copy(color, 2, delta).start()
    for c in grid_copies(2):
        c.wait()
    for late in ([1], [0, 1]):
        for delta in OTHERS:
            for color in range(3):
                if goes(color, 2, delta) and travelled(color, 2, delta) == late:
                    copy(color, 1, delta).wait_recv()
                    copy(color, 2, delta).start()
    for row in range(32):
        router_ref[:, row * width : (row + 1) * width] = grid[row // 8, (row // 2) % 4, row % 2]

    for phase in range(3):
        for delta in OTHERS:
            for color in range(3):
                if goes(color, phase, delta):
                    if is_final(color, phase, delta):
                        copy(color, phase, delta).wait_recv()
                    copy(color, phase, delta).wait_send()


def solution(mesh):
    def shards(master_down, router_weight, router_gain):
        experts, long, width = master_down.shape
        n = mesh.shape["rows"]
        depth = long // n
        cuts = cuts_of(depth, 3, 8)
        block = (n, experts, depth, width)
        dma = pltpu.SemaphoreType.DMA
        final, router = pl.pallas_call(
            functools.partial(kernel, "rows", "owner", cuts),
            out_shape=(
                pltpu.VMEM((experts, depth, n * width), jnp.bfloat16),
                pltpu.VMEM((experts * OWNERS, n * width), jnp.bfloat16),
            ),
            in_specs=[
                pl.BlockSpec(memory_space=pl.ANY),
                pl.BlockSpec(memory_space=pltpu.VMEM),
                pl.BlockSpec(memory_space=pltpu.VMEM),
            ],
            out_specs=(pl.BlockSpec(memory_space=pltpu.VMEM), pl.BlockSpec(memory_space=pltpu.VMEM)),
            scratch_shapes=[
                pltpu.VMEM(block, jnp.float32),
                pltpu.VMEM(block, jnp.bfloat16),
                pltpu.VMEM(block, jnp.bfloat16),
                pltpu.VMEM(block, jnp.bfloat16),
                pltpu.VMEM((OWNERS, 8, width), jnp.bfloat16),
                pltpu.VMEM((*SIZES, 8, width), jnp.bfloat16),
                dma((n,)),
                dma((3, 3, n)),
                dma((3, 3, n)),
                dma((OWNERS,)),
                dma((OWNERS,)),
                dma((3, 4)),
                dma((3, 4)),
            ],
            compiler_params=pltpu.CompilerParams(
                collective_id=0, has_side_effects=True, vmem_limit_bytes=48 * 2**20
            ),
        )(master_down, router_weight.T, router_gain.reshape(1, width))
        return jnp.swapaxes(final, 1, 2), router.T

    return jax.shard_map(
        shards,
        mesh=mesh,
        in_specs=(P("owner", None, "rows"), P("rows", "owner"), P("rows")),
        out_specs=(P("owner", None, "rows"), P()),
        check_vma=False,
    )
```

time: 144 us -> 100 us (0.69); the launches traced: 142 us -> 100 us
  Pallas kernels: 0 us -> 95.7 us
  waiting for transfers between devices: 45.2 us -> 0 us
  blocking collectives: 43.4 us -> 0 us
  starting transfers between devices: 28.9 us -> 0 us
  other arithmetic: 13.2 us -> 0 us
  local copies, waits for them, and re-layouts: 10.5 us -> 3.68 us
    pallas_call x0 -> x1, Pallas kernels: none -> 95.7 us  [shards(): pl.pallas_call(functools.partial(kernel, 'rows', 'owner', cuts), out_shap...]
    all_to_all x3 -> x0, waiting for transfers between devices: 45.2 us -> none  [the longest x2 45.2 us: cut_exchange(): lax.all_to_all(slab, axis, split_axis=0, concat_axis=0, tiled=True)]
    all_gather x2 -> x0, blocking collectives: 43.4 us -> none  [all_blocks(): blocks = lax.all_gather(blocks, axes[k])]
    all_to_all x3 -> x0, starting transfers between devices: 28.9 us -> none  [the longest x2 18 us: cut_exchange(): lax.all_to_all(slab, axis, split_axis=0, concat_axis=0, tiled=True)]
    split x3 -> x0, local copies, waits for them, and re-layouts: 9.21 us -> none  [cut_exchange(): jnp.split(blocks, edges_of(blocks.shape[split_at], pieces), axis=split_at)]
    transpose x1 -> x0, other arithmetic: 6.65 us -> none  [shards(): final_down = jnp.transpose(final_down, (0, 2, 1))]
    convert_element_type x2 -> x0, other arithmetic: 6.5 us -> none  [the longest x1 5.81 us: shards(): narrow_down = master_down.astype(jnp.bfloat16)]
    unnamed x0 -> x2, local copies, waits for them, and re-layouts: none -> 3.68 us
  transfers between devices with their start and end apart: 3 -> 0, of which waited for: 2 -> 0; matrix products, arithmetic and copies ran while one was open for 11% -> 0% of each run, Pallas kernels for 0% -> 0%
where the time goes in v1:
time: 100 us
  Pallas kernels  95.7 us (96%)
  local copies, waits for them, and re-layouts  3.68 us (4%)
    pallas_call x1, Pallas kernels, shards(): pl.pallas_call(functools.partial(kernel, 'rows', 'owner', cuts), out_shap...  95.7 us
    unnamed x2, local copies, waits for them, and re-layouts  3.68 us

profile of v1, /device:TPU:0, one launch (start us, length us, event | category | flops | bytes accessed | tf_op | source)
XLA Modules:
  0.0 100.1 jit_solution(12658535432940178905)
XLA Ops:
  0.6 95.7 %shard_map.50 = (bf16[2,448,4096]{2,1,0:T(8,128)(2,1)S(1)}, bf16[8,4096]{1,0:T(8,128)(2,1)S(1)}) custom-call(f32[2,14336,128]{2,1,0:T(8,128)} %x_ref.1, f32[2,128]{1,0:T(2,128)} %bitcast.6, f32[1,128]{1,0:T(1,128)} %bitcast.7), custom_call_target="tpu_custom_call" | custom-call | tf_op jit(solution)/shard_map/pallas_call | solution.py:211
  96.4 3.1 %copy.7 = bf16[2,4096,448]{1,2,0:T(8,128)(2,1)} copy(bf16[2,4096,448]{1,2,0:T(8,128)(2,1)S(1)} %bitcast.4) | data formatting | bytes 14680064
  99.4 0.6 copy.8

commit v2 on v1

v2 whole, which is shorter than its diff:
```python
import functools
import itertools

import jax
import jax.numpy as jnp
from jax import lax
from jax.experimental import pallas as pl
from jax.experimental.pallas import tpu as pltpu
from jax.sharding import PartitionSpec as P

MESH = pl.DeviceIdType.MESH
SIZES = (4, 4, 2)
ORDERS = ((0, 1, 2), (1, 2, 0), (2, 0, 1))
COLORS = range(3)
OWNERS = 4
STEPS = {2: (1,), 4: (1, 3, 2)}


def cuts_of(length, count, step):
    tiles = length // step
    edges = [tiles * k // count * step for k in range(count)] + [length]
    return [(a, b - a) for a, b in zip(edges, edges[1:])]


class Move:
    def __init__(self, color, phase, box):
        self.color, self.phase = color, phase
        self.box = tuple(box[k] for k in range(3))
        self.dim = ORDERS[color][phase]
        self.step = self.box[self.dim][0]
        self.index = None

    def deltas(self):
        return list(itertools.product(*(range(a, a + n) for a, n in self.box)))

    def origin(self):
        found = {
            max((q for q in range(self.phase) if d[ORDERS[self.color][q]]), default=None, key=lambda q: q)
            for d in self.deltas()
        }
        (phase,) = found
        return phase


def plan():
    def move(color, phase, a, b, c):
        dims = ORDERS[color]
        return Move(color, phase, {dims[0]: a, dims[1]: b, dims[2]: c})

    def sizes(color):
        return [SIZES[d] for d in ORDERS[color]]

    rest, zero = lambda n: (1, n - 1), (0, 1)
    first, second, third = [], [], []
    for color in COLORS:
        na, nb, nc = sizes(color)
        starts, ends = [], []
        for a in STEPS[na]:
            bs = [rest(nb)] if na == 4 else [(b, 1) for b in STEPS[nb]]
            starts += [move(color, 0, (a, 1), b, (0, nc)) for b in bs]
            ends.append(move(color, 0, (a, 1), zero, (0, nc)))
        first.append(starts + ends)
        second.append(
            [[move(color, 1, zero, (b, 1), (0, nc)) for b in STEPS[nb]]]
            + [[move(color, 1, (a, 1), (b, 1), (0, nc)) for b in STEPS[nb]] for a in STEPS[na]]
        )
        third.append(
            [[move(color, 2, zero, zero, (c, 1)) for c in STEPS[nc]]]
            + [[move(color, 2, rest(na), zero, (c, 1)) for c in STEPS[nc]]]
            + [[move(color, 2, (0, na), (b, 1), (c, 1)) for c in STEPS[nc]] for b in STEPS[nb]]
        )

    def woven(lists):
        return [m for row in itertools.zip_longest(*lists) for m in row if m is not None]

    def woven_rows(lists):
        return [m for row in itertools.zip_longest(*lists) for part in row if part for m in woven([part])]

    stages = (
        woven(first),
        woven([rows[0] for rows in second]),
        woven_rows([rows[1:] for rows in second]),
        woven([rows[0] + rows[1] for rows in third]),
        woven_rows([rows[2:] for rows in third]),
    )
    for k, m in enumerate(itertools.chain(*stages)):
        m.index = k
    return stages


STAGES = plan()
MOVES = list(itertools.chain(*STAGES))
BROUGHT = {(m.color, m.phase, d): m for m in MOVES for d in m.deltas()}
HEAD = 8


def kernel(cuts, x_ref, w_ref, g_ref, out_ref, router_ref, *scratch):
    loaded, held, *relays = (scratch[3 * k : 3 * k + 3] for k in range(5))
    parts, grid, load_sem, send_sem, recv_sem, part_send, part_recv, grid_send, grid_recv = scratch[15:]
    me = lax.axis_index("rows")
    own = lax.axis_index("owner")
    place = (me // 8, (me // 2) % 4, me % 2)
    depth = out_ref.shape[1]
    width = w_ref.shape[1]

    def moved(delta, sign=1):
        z, y, x = (lax.rem(p + sign * d + s, s) if d else p for p, d, s in zip(place, delta, SIZES))
        return (z * SIZES[1] + y) * SIZES[2] + x

    peers = {
        (dim, k): moved([k if d == dim else 0 for d in range(3)]) for dim in range(3) for k in range(1, SIZES[dim])
    }
    mates = [lax.rem(own + k, OWNERS) for k in range(OWNERS)]

    barrier = pltpu.get_barrier_semaphore()
    for peer in peers.values():
        pl.semaphore_signal(barrier, inc=1, device_id=(own, peer), device_id_type=MESH)
    for k in range(1, OWNERS):
        pl.semaphore_signal(barrier, inc=1, device_id=(mates[k], me), device_id_type=MESH)

    def load(color, delta):
        start, size = cuts[color]
        top = pl.multiple_of(moved(delta) * depth + start, 8)
        flat = (delta[0] * SIZES[1] + delta[1]) * SIZES[2] + delta[2]
        return pltpu.make_async_copy(
            x_ref.at[:, pl.ds(top, size), :], loaded[color].at[delta], load_sem.at[color, flat]
        )

    own_moves = [m for m in MOVES if m.origin() is None]
    here = (0, 0, 0)
    for m in own_moves:
        for delta in m.deltas():
            load(m.color, delta).start()
    for color in COLORS:
        load(color, here).start()

    def column(delta):
        return pl.ds(pl.multiple_of(moved(delta, -1) * width, 128), width)

    def cast(m):
        for delta in m.deltas():
            load(m.color, delta).wait()
            held[m.color][delta] = loaded[m.color][delta].astype(jnp.bfloat16)

    def copy(m):
        origin = m.origin()
        box = tuple(pl.ds(a, n) for a, n in m.box)
        source = held if origin is None else relays[origin]
        return pltpu.make_async_remote_copy(
            src_ref=source[m.color].at[box],
            dst_ref=relays[m.phase][m.color].at[box],
            send_sem=send_sem.at[m.index],
            recv_sem=recv_sem.at[m.index],
            device_id=(own, peers[m.dim, m.step]),
            device_id_type=MESH,
        )

    arrived = set()

    def await_arrival(m):
        if m.index in arrived:
            return
        arrived.add(m.index)
        copy(m).wait_recv()
        ended.extend((m, d) for d in m.deltas() if not any(d[ORDERS[m.color][q]] for q in range(m.phase + 1, 3)))

    ended = []

    def settle():
        for m, delta in ended:
            start, size = cuts[m.color]
            out_ref[:, pl.ds(start, size), column(delta)] = relays[m.phase][m.color][delta]
        ended.clear()

    def needs(m):
        origin = m.origin()
        if origin is None:
            return []
        wanted = {BROUGHT[m.color, origin, d].index for d in m.deltas()}
        return [MOVES[k] for k in sorted(wanted)]

    scaled = (w_ref[...] * g_ref[...]).astype(jnp.bfloat16).astype(jnp.float32)
    line = lax.broadcasted_iota(jnp.int32, (8, width), 0)
    pair = jnp.where(
        line % 2 == 0, jnp.broadcast_to(scaled[0:1, :], (8, width)), jnp.broadcast_to(scaled[1:2, :], (8, width))
    )
    parts[0] = pair.astype(jnp.bfloat16)

    def part_copy(k):
        return pltpu.make_async_remote_copy(
            src_ref=parts.at[0], dst_ref=parts.at[k], send_sem=part_send.at[k], recv_sem=part_recv.at[k],
            device_id=(mates[k], me), device_id_type=MESH)

    def grid_copies(dim):
        if dim == 0:
            block = grid.at[place[0], place[1], place[2]]
        elif dim == 1:
            block = grid.at[:, place[1], place[2]]
        else:
            block = grid.at[:, :, place[2]]
        return [
            pltpu.make_async_remote_copy(
                src_ref=block, dst_ref=block, send_sem=grid_send.at[dim, k], recv_sem=grid_recv.at[dim, k],
                device_id=(own, peers[dim, k]), device_id_type=MESH)
            for k in range(1, SIZES[dim])
        ]

    starts = STAGES[0]
    for m in starts[:HEAD]:
        cast(m)
    pl.semaphore_wait(barrier, len(peers) + OWNERS - 1)
    for k in range(1, OWNERS):
        part_copy(k).start()
    for m in starts[:HEAD]:
        copy(m).start()
    previous = None
    for m in starts[HEAD:]:
        cast(m)
        if previous is not None:
            copy(previous).start()
        previous = m
    for k in range(1, OWNERS):
        part_copy(k).wait()
    tile = parts[0].astype(jnp.float32)
    for k in range(1, OWNERS):
        theirs = lax.rem(own - k + OWNERS, OWNERS)
        tile = jnp.where(line // 2 == theirs, parts[k].astype(jnp.float32), tile)
    grid[place[0], place[1], place[2]] = tile.astype(jnp.bfloat16)
    for m in STAGES[1]:
        cast(m)
        if previous is not None:
            copy(previous).start()
        previous = m
    for c in grid_copies(0):
        c.start()
    for m in STAGES[3]:
        if m.origin() is None:
            cast(m)
    copy(previous).start()
    for color in COLORS:
        start, size = cuts[color]
        load(color, here).wait()
        out_ref[:, pl.ds(start, size), column(here)] = loaded[color][here].astype(jnp.bfloat16)

    half = len(STAGES[2]) // 2
    for k, m in enumerate(STAGES[2]):
        for n in needs(m):
            await_arrival(n)
        copy(m).start()
        if k == half:
            for c in grid_copies(0):
                c.wait()
            for c in grid_copies(1):
                c.start()
    for m in STAGES[3]:
        for n in needs(m):
            await_arrival(n)
        copy(m).start()
    for m in starts:
        await_arrival(m)
    settle()
    late = len(STAGES[4]) - 3
    for k, m in enumerate(STAGES[4]):
        for n in needs(m):
            await_arrival(n)
        copy(m).start()
        if k == 0:
            for c in grid_copies(1):
                c.wait()
            for c in grid_copies(2):
                c.start()
    settle()
    for m in MOVES[: len(STAGES[0]) + len(STAGES[1]) + len(STAGES[2])]:
        copy(m).wait_send()
    for c in grid_copies(2):
        c.wait()
    for row in range(32):
        router_ref[:, row * width : (row + 1) * width] = grid[row // 8, (row // 2) % 4, row % 2]
    for m in STAGES[3] + STAGES[4]:
        await_arrival(m)
        settle()
    for m in STAGES[3] + STAGES[4]:
        copy(m).wait_send()


def drain(final_ref, router_ref, final_out, router_out, sems):
    pieces = 8
    height = final_ref.shape[1] // pieces
    copies = [
        pltpu.make_async_copy(
            final_ref.at[e, pl.ds(k * height, height)], final_out.at[e, pl.ds(k * height, height)], sems.at[e * pieces + k]
        )
        for e in range(final_ref.shape[0])
        for k in range(pieces)
    ]
    copies.append(pltpu.make_async_copy(router_ref, router_out, sems.at[len(copies)]))
    for c in copies:
        c.start()
    for c in copies:
        c.wait()


def solution(mesh):
    def shards(master_down, router_weight, router_gain):
        experts, long, width = master_down.shape
        n = mesh.shape["rows"]
        depth = long // n
        cuts = cuts_of(depth, 3, 16)
        dma = pltpu.SemaphoreType.DMA
        blocks = [(*SIZES, experts, size, width) for _, size in cuts]
        final, router = pl.pallas_call(
            functools.partial(kernel, cuts),
            out_shape=(
                pltpu.VMEM((experts, depth, n * width), jnp.bfloat16),
                pltpu.VMEM((experts * OWNERS, n * width), jnp.bfloat16),
            ),
            in_specs=[
                pl.BlockSpec(memory_space=pl.ANY),
                pl.BlockSpec(memory_space=pltpu.VMEM),
                pl.BlockSpec(memory_space=pltpu.VMEM),
            ],
            out_specs=(pl.BlockSpec(memory_space=pltpu.VMEM), pl.BlockSpec(memory_space=pltpu.VMEM)),
            scratch_shapes=[pltpu.VMEM(b, jnp.float32) for b in blocks]
            + [pltpu.VMEM(b, jnp.bfloat16) for _ in range(4) for b in blocks]
            + [
                pltpu.VMEM((OWNERS, 8, width), jnp.bfloat16),
                pltpu.VMEM((*SIZES, 8, width), jnp.bfloat16),
                dma((3, n)),
                dma((len(MOVES),)),
                dma((len(MOVES),)),
                dma((OWNERS,)),
                dma((OWNERS,)),
                dma((3, 4)),
                dma((3, 4)),
            ],
            compiler_params=pltpu.CompilerParams(
                collective_id=0, has_side_effects=True, vmem_limit_bytes=48 * 2**20
            ),
        )(master_down, router_weight.T, router_gain.reshape(1, width))
        final, router = pl.pallas_call(
            drain,
            out_shape=(
                jax.ShapeDtypeStruct(final.shape, final.dtype),
                jax.ShapeDtypeStruct(router.shape, router.dtype),
            ),
            in_specs=[pl.BlockSpec(memory_space=pl.ANY)] * 2,
            out_specs=(pl.BlockSpec(memory_space=pl.ANY), pl.BlockSpec(memory_space=pl.ANY)),
            scratch_shapes=[dma((17,))],
            compiler_params=pltpu.CompilerParams(vmem_limit_bytes=2**20),
        )(final, router)
        return jnp.swapaxes(final, 1, 2), router.T

    return jax.shard_map(
        shards,
        mesh=mesh,
        in_specs=(P("owner", None, "rows"), P("rows", "owner"), P("rows")),
        out_specs=(P("owner", None, "rows"), P()),
        check_vma=False,
    )
```

time: 100 us -> 94.3 us (0.943)
  local copies, waits for them, and re-layouts: 3.68 us -> 0 us
  Pallas kernels: 95.7 us -> 93.5 us
    unnamed x2 -> x0, local copies, waits for them, and re-layouts: 3.68 us -> none
    pallas_call x1 -> x2, Pallas kernels: 95.7 us -> 93.5 us  [the longest x1 90.4 us: shards(): pl.pallas_call(functools.partial(kernel, cuts), out_shape=(pltpu.VMEM((ex...]
where the time goes in v2:
time: 94.3 us; the launch traced here: 94.1 us
  Pallas kernels  93.5 us (99%)
    pallas_call x1, Pallas kernels, shards(): pl.pallas_call(functools.partial(kernel, cuts), out_shape=(pltpu.VMEM((ex...  90.4 us
    pallas_call x1, Pallas kernels, shards(): pl.pallas_call(drain, out_shape=(jax.ShapeDtypeStruct(final.shape, final....  3.12 us

profile of v2, /device:TPU:0, one launch (start us, length us, event | category | flops | bytes accessed | tf_op | source)
XLA Modules:
  0.0 94.1 jit_solution(3498556771006212591)
XLA Ops:
  0.6 90.4 %shard_map.50 = (bf16[2,448,4096]{2,1,0:T(8,128)(2,1)S(1)}, bf16[8,4096]{1,0:T(8,128)(2,1)S(1)}) custom-call(f32[2,14336,128]{2,1,0:T(8,128)} %x_ref.1, f32[2,128]{1,0:T(2,128)} %bitcast.4, f32[1,128]{1,0:T(1,128)} %bitcast.5), custom_call_target="tpu_custom_call" | custom-call | tf_op jit(solution)/shard_map/pallas_call | solution.py:311
  91.0 3.1 %shard_map.51 = (bf16[2,448,4096]{2,1,0:T(8,128)(2,1)}, bf16[8,4096]{1,0:T(8,128)(2,1)}) custom-call(bf16[2,448,4096]{2,1,0:T(8,128)(2,1)S(1)} %get-tuple-element.6.final_ref, bf16[8,4096]{1,0:T(8,128)(2,1)S(1)} %get-tuple-element.7.router_ref), custom_call_target="tpu_custom_call" | custom-call | tf_op jit(solution)/shard_map/pallas_call | solution.py:340

commit v3 on v2

--- a/solution.py
+++ b/solution.py
@@ -23,65 +23,50 @@
 
 
 class Move:
-    def __init__(self, color, phase, box):
-        self.color, self.phase = color, phase
+    def __init__(self, color, phase, boxes, direct=False):
+        self.color, self.phase, self.direct = color, phase, direct
+        box = dict(zip(ORDERS[color], boxes))
         self.box = tuple(box[k] for k in range(3))
         self.dim = ORDERS[color][phase]
         self.step = self.box[self.dim][0]
+        self.source = None if phase == 0 else 0 if phase == 1 or boxes[1] == (0, 1) else 1
         self.index = None
 
     def deltas(self):
         return list(itertools.product(*(range(a, a + n) for a, n in self.box)))
 
-    def origin(self):
-        found = {
-            max((q for q in range(self.phase) if d[ORDERS[self.color][q]]), default=None, key=lambda q: q)
-            for d in self.deltas()
-        }
-        (phase,) = found
-        return phase
+    def brought(self, delta):
+        return max((q for q in range(self.phase) if delta[ORDERS[self.color][q]]), default=None)
 
 
 def plan():
-    def move(color, phase, a, b, c):
-        dims = ORDERS[color]
-        return Move(color, phase, {dims[0]: a, dims[1]: b, dims[2]: c})
-
-    def sizes(color):
-        return [SIZES[d] for d in ORDERS[color]]
-
-    rest, zero = lambda n: (1, n - 1), (0, 1)
-    first, second, third = [], [], []
+    zero = (0, 1)
+    first, second, third, fourth = [], [], [], []
     for color in COLORS:
-        na, nb, nc = sizes(color)
-        starts, ends = [], []
-        for a in STEPS[na]:
-            bs = [rest(nb)] if na == 4 else [(b, 1) for b in STEPS[nb]]
-            starts += [move(color, 0, (a, 1), b, (0, nc)) for b in bs]
-            ends.append(move(color, 0, (a, 1), zero, (0, nc)))
-        first.append(starts + ends)
-        second.append(
-            [[move(color, 1, zero, (b, 1), (0, nc)) for b in STEPS[nb]]]
-            + [[move(color, 1, (a, 1), (b, 1), (0, nc)) for b in STEPS[nb]] for a in STEPS[na]]
-        )
-        third.append(
-            [[move(color, 2, zero, zero, (c, 1)) for c in STEPS[nc]]]
-            + [[move(color, 2, rest(na), zero, (c, 1)) for c in STEPS[nc]]]
-            + [[move(color, 2, (0, na), (b, 1), (c, 1)) for c in STEPS[nc]] for b in STEPS[nb]]
-        )
+        na, nb, nc = (SIZES[d] for d in ORDERS[color])
+        halves = [(0, nb // 2), (nb // 2, nb - nb // 2)] if na == 2 else [(0, nb)]
+        first.append([Move(color, 0, ((a, 1), b, (0, nc))) for a in STEPS[na] for b in halves])
+        second.append([Move(color, 1, (zero, (b, 1), (0, nc))) for b in STEPS[nb]])
+        third.append([Move(color, 1, ((1, na - 1), (b, 1), (0, nc))) for b in STEPS[nb]])
+        early = [Move(color, 2, ((0, na), zero, (c, 1))) for c in STEPS[nc]]
+        groups = [(b, 1) for b in STEPS[nb]] if nc == 2 else [(1, nb - 1)]
+        late = [((0, na), b, (c, 1)) for c in STEPS[nc] for b in groups]
+        last = [
+            Move(color, 2, ((a, 1), (b, 1), late[-1][2]), True)
+            for b in range(late[-1][1][0], sum(late[-1][1]))
+            for a in range(na)
+        ]
+        fourth.append((early, [Move(color, 2, boxes) for boxes in late[:-1]] + last))
 
     def woven(lists):
         return [m for row in itertools.zip_longest(*lists) for m in row if m is not None]
 
-    def woven_rows(lists):
-        return [m for row in itertools.zip_longest(*lists) for part in row if part for m in woven([part])]
-
     stages = (
         woven(first),
-        woven([rows[0] for rows in second]),
-        woven_rows([rows[1:] for rows in second]),
-        woven([rows[0] + rows[1] for rows in third]),
-        woven_rows([rows[2:] for rows in third]),
+        woven(second),
+        woven(third),
+        woven([early for early, _ in fourth]),
+        woven([late for _, late in fourth]),
     )
     for k, m in enumerate(itertools.chain(*stages)):
         m.index = k
@@ -91,7 +76,7 @@
 STAGES = plan()
 MOVES = list(itertools.chain(*STAGES))
 BROUGHT = {(m.color, m.phase, d): m for m in MOVES for d in m.deltas()}
-HEAD = 8
+HEAD = 3
 
 
 def kernel(cuts, x_ref, w_ref, g_ref, out_ref, router_ref, *scratch):
@@ -126,11 +111,11 @@
             x_ref.at[:, pl.ds(top, size), :], loaded[color].at[delta], load_sem.at[color, flat]
         )
 
-    own_moves = [m for m in MOVES if m.origin() is None]
     here = (0, 0, 0)
-    for m in own_moves:
+    for m in MOVES:
         for delta in m.deltas():
-            load(m.color, delta).start()
+            if m.brought(delta) is None:
+                load(m.color, delta).start()
     for color in COLORS:
         load(color, here).start()
 
@@ -138,17 +123,27 @@
         return pl.ds(pl.multiple_of(moved(delta, -1) * width, 128), width)
 
     def cast(m):
+        target = held if m.source is None else relays[0]
         for delta in m.deltas():
-            load(m.color, delta).wait()
-            held[m.color][delta] = loaded[m.color][delta].astype(jnp.bfloat16)
+            if m.brought(delta) is None:
+                load(m.color, delta).wait()
+                target[m.color][delta] = loaded[m.color][delta].astype(jnp.bfloat16)
 
     def copy(m):
-        origin = m.origin()
-        box = tuple(pl.ds(a, n) for a, n in m.box)
-        source = held if origin is None else relays[origin]
+        source = (held if m.source is None else relays[m.source])[m.color]
+        target = relays[m.phase][m.color]
+        if m.direct:
+            (delta,) = m.deltas()
+            start, size = cuts[m.color]
+            dims = ORDERS[m.color]
+            gone = tuple(0 if k == dims[2] else delta[k] for k in range(3))
+            source, target = source.at[delta], out_ref.at[:, pl.ds(start, size), column(gone)]
+        else:
+            box = tuple(pl.ds(a, n) for a, n in m.box)
+            source, target = source.at[box], target.at[box]
         return pltpu.make_async_remote_copy(
-            src_ref=source[m.color].at[box],
-            dst_ref=relays[m.phase][m.color].at[box],
+            src_ref=source,
+            dst_ref=target,
             send_sem=send_sem.at[m.index],
             recv_sem=recv_sem.at[m.index],
             device_id=(own, peers[m.dim, m.step]),
@@ -162,6 +157,8 @@
             return
         arrived.add(m.index)
         copy(m).wait_recv()
+        if m.direct:
+            return
         ended.extend((m, d) for d in m.deltas() if not any(d[ORDERS[m.color][q]] for q in range(m.phase + 1, 3)))
 
     ended = []
@@ -173,10 +170,8 @@
         ended.clear()
 
     def needs(m):
-        origin = m.origin()
-        if origin is None:
-            return []
-        wanted = {BROUGHT[m.color, origin, d].index for d in m.deltas()}
+        came = {(m.brought(d), d) for d in m.deltas()}
+        wanted = {BROUGHT[m.color, q, d].index for q, d in came if q is not None}
         return [MOVES[k] for k in sorted(wanted)]
 
     scaled = (w_ref[...] * g_ref[...]).astype(jnp.bfloat16).astype(jnp.float32)
@@ -219,38 +214,33 @@
         if previous is not None:
             copy(previous).start()
         previous = m
-    for k in range(1, OWNERS):
-        part_copy(k).wait()
-    tile = parts[0].astype(jnp.float32)
-    for k in range(1, OWNERS):
-        theirs = lax.rem(own - k + OWNERS, OWNERS)
-        tile = jnp.where(line // 2 == theirs, parts[k].astype(jnp.float32), tile)
-    grid[place[0], place[1], place[2]] = tile.astype(jnp.bfloat16)
     for m in STAGES[1]:
         cast(m)
         if previous is not None:
             copy(previous).start()
         previous = m
-    for c in grid_copies(0):
-        c.start()
     for m in STAGES[3]:
-        if m.origin() is None:
-            cast(m)
+        cast(m)
     copy(previous).start()
     for color in COLORS:
         start, size = cuts[color]
         load(color, here).wait()
         out_ref[:, pl.ds(start, size), column(here)] = loaded[color][here].astype(jnp.bfloat16)
 
-    half = len(STAGES[2]) // 2
     for k, m in enumerate(STAGES[2]):
         for n in needs(m):
             await_arrival(n)
         copy(m).start()
-        if k == half:
+        if k == 0:
+            for j in range(1, OWNERS):
+                part_copy(j).wait()
+            tile = parts[0].astype(jnp.float32)
+            for j in range(1, OWNERS):
+                theirs = lax.rem(own - j + OWNERS, OWNERS)
+                tile = jnp.where(line // 2 == theirs, parts[j].astype(jnp.float32), tile)
+            grid[place[0], place[1], place[2]] = tile.astype(jnp.bfloat16)
+        if k == 1:
             for c in grid_copies(0):
-                c.wait()
-            for c in grid_copies(1):
                 c.start()
     for m in STAGES[3]:
         for n in needs(m):
@@ -259,12 +249,15 @@
     for m in starts:
         await_arrival(m)
     settle()
-    late = len(STAGES[4]) - 3
+    for c in grid_copies(0):
+        c.wait()
+    for c in grid_copies(1):
+        c.start()
     for k, m in enumerate(STAGES[4]):
         for n in needs(m):
             await_arrival(n)
         copy(m).start()
-        if k == 0:
+        if k == 5:
             for c in grid_copies(1):
                 c.wait()
             for c in grid_copies(2):

time: 94.3 us -> 93.7 us (level)
  no operation moved by 1% of the time
where the time goes in v3:
time: 93.7 us; the launch traced here: 93.6 us
  Pallas kernels  93 us (99%)
    pallas_call x1, Pallas kernels, shards(): pl.pallas_call(functools.partial(kernel, cuts), out_shape=(pltpu.VMEM((ex...  89.8 us
    pallas_call x1, Pallas kernels, shards(): pl.pallas_call(drain, out_shape=(jax.ShapeDtypeStruct(final.shape, final....  3.12 us

profile of v3, /device:TPU:0, one launch (start us, length us, event | category | flops | bytes accessed | tf_op | source)
XLA Modules:
  0.0 93.6 jit_solution(8044905775676282826)
XLA Ops:
  0.6 89.8 %shard_map.50 = (bf16[2,448,4096]{2,1,0:T(8,128)(2,1)S(1)}, bf16[8,4096]{1,0:T(8,128)(2,1)S(1)}) custom-call(f32[2,14336,128]{2,1,0:T(8,128)} %x_ref.1, f32[2,128]{1,0:T(2,128)} %bitcast.4, f32[1,128]{1,0:T(1,128)} %bitcast.5), custom_call_target="tpu_custom_call" | custom-call | tf_op jit(solution)/shard_map/pallas_call | solution.py:304
  90.5 3.1 %shard_map.51 = (bf16[2,448,4096]{2,1,0:T(8,128)(2,1)}, bf16[8,4096]{1,0:T(8,128)(2,1)}) custom-call(bf16[2,448,4096]{2,1,0:T(8,128)(2,1)S(1)} %get-tuple-element.6.final_ref, bf16[8,4096]{1,0:T(8,128)(2,1)S(1)} %get-tuple-element.7.router_ref), custom_call_target="tpu_custom_call" | custom-call | tf_op jit(solution)/shard_map/pallas_call | solution.py:333

commit v4 on v3

--- a/solution.py
+++ b/solution.py
@@ -81,12 +81,12 @@
 
 def kernel(cuts, x_ref, w_ref, g_ref, out_ref, router_ref, *scratch):
     loaded, held, *relays = (scratch[3 * k : 3 * k + 3] for k in range(5))
-    parts, grid, load_sem, send_sem, recv_sem, part_send, part_recv, grid_send, grid_recv = scratch[15:]
+    weight, gain, small_sem, parts, grid, load_sem, send_sem, recv_sem, part_send, part_recv, grid_send, grid_recv = scratch[15:]
     me = lax.axis_index("rows")
     own = lax.axis_index("owner")
     place = (me // 8, (me // 2) % 4, me % 2)
     depth = out_ref.shape[1]
-    width = w_ref.shape[1]
+    width = weight.shape[1]
 
     def moved(delta, sign=1):
         z, y, x = (lax.rem(p + sign * d + s, s) if d else p for p, d, s in zip(place, delta, SIZES))
@@ -97,6 +97,12 @@
     }
     mates = [lax.rem(own + k, OWNERS) for k in range(OWNERS)]
 
+    small = [
+        pltpu.make_async_copy(w_ref, weight, small_sem.at[0]),
+        pltpu.make_async_copy(g_ref, gain, small_sem.at[1]),
+    ]
+    for c in small:
+        c.start()
     barrier = pltpu.get_barrier_semaphore()
     for peer in peers.values():
         pl.semaphore_signal(barrier, inc=1, device_id=(own, peer), device_id_type=MESH)
@@ -174,12 +180,7 @@
         wanted = {BROUGHT[m.color, q, d].index for q, d in came if q is not None}
         return [MOVES[k] for k in sorted(wanted)]
 
-    scaled = (w_ref[...] * g_ref[...]).astype(jnp.bfloat16).astype(jnp.float32)
     line = lax.broadcasted_iota(jnp.int32, (8, width), 0)
-    pair = jnp.where(
-        line % 2 == 0, jnp.broadcast_to(scaled[0:1, :], (8, width)), jnp.broadcast_to(scaled[1:2, :], (8, width))
-    )
-    parts[0] = pair.astype(jnp.bfloat16)
 
     def part_copy(k):
         return pltpu.make_async_remote_copy(
@@ -203,6 +204,13 @@
     starts = STAGES[0]
     for m in starts[:HEAD]:
         cast(m)
+    for c in small:
+        c.wait()
+    scaled = (weight[...] * gain[...]).astype(jnp.bfloat16).astype(jnp.float32)
+    pair = jnp.where(
+        line % 2 == 0, jnp.broadcast_to(scaled[0:1, :], (8, width)), jnp.broadcast_to(scaled[1:2, :], (8, width))
+    )
+    parts[0] = pair.astype(jnp.bfloat16)
     pl.semaphore_wait(barrier, len(peers) + OWNERS - 1)
     for k in range(1, OWNERS):
         part_copy(k).start()
@@ -298,7 +306,7 @@
         experts, long, width = master_down.shape
         n = mesh.shape["rows"]
         depth = long // n
-        cuts = cuts_of(depth, 3, 16)
+        cuts = cuts_of(depth, 3, 8)
         dma = pltpu.SemaphoreType.DMA
         blocks = [(*SIZES, experts, size, width) for _, size in cuts]
         final, router = pl.pallas_call(
@@ -307,15 +315,14 @@
                 pltpu.VMEM((experts, depth, n * width), jnp.bfloat16),
                 pltpu.VMEM((experts * OWNERS, n * width), jnp.bfloat16),
             ),
-            in_specs=[
-                pl.BlockSpec(memory_space=pl.ANY),
-                pl.BlockSpec(memory_space=pltpu.VMEM),
-                pl.BlockSpec(memory_space=pltpu.VMEM),
-            ],
+            in_specs=[pl.BlockSpec(memory_space=pl.ANY)] * 3,
             out_specs=(pl.BlockSpec(memory_space=pltpu.VMEM), pl.BlockSpec(memory_space=pltpu.VMEM)),
             scratch_shapes=[pltpu.VMEM(b, jnp.float32) for b in blocks]
             + [pltpu.VMEM(b, jnp.bfloat16) for _ in range(4) for b in blocks]
             + [
+                pltpu.VMEM((2, width), jnp.float32),
+                pltpu.VMEM((1, width), jnp.float32),
+                dma((2,)),
                 pltpu.VMEM((OWNERS, 8, width), jnp.bfloat16),
                 pltpu.VMEM((*SIZES, 8, width), jnp.bfloat16),
                 dma((3, n)),

time: 93.7 us -> 93.1 us (level)
  no operation moved by 1% of the time
where the time goes in v4:
time: 93.1 us; the launch traced here: 93 us
  Pallas kernels  92.3 us (99%)
    pallas_call x1, Pallas kernels, shards(): pl.pallas_call(functools.partial(kernel, cuts), out_shape=(pltpu.VMEM((ex...  89.2 us
    pallas_call x1, Pallas kernels, shards(): pl.pallas_call(drain, out_shape=(jax.ShapeDtypeStruct(final.shape, final....  3.12 us

profile of v4, /device:TPU:0, one launch (start us, length us, event | category | flops | bytes accessed | tf_op | source)
XLA Modules:
  0.0 93.0 jit_solution(7105097862034183449)
XLA Ops:
  0.6 89.2 %shard_map.50 = (bf16[2,448,4096]{2,1,0:T(8,128)(2,1)S(1)}, bf16[8,4096]{1,0:T(8,128)(2,1)S(1)}) custom-call(f32[2,14336,128]{2,1,0:T(8,128)} %x_ref.1, f32[2,128]{1,0:T(2,128)} %bitcast.4, f32[1,128]{1,0:T(1,128)} %bitcast.5), custom_call_target="tpu_custom_call" | custom-call | tf_op jit(solution)/shard_map/pallas_call | solution.py:312
  89.9 3.1 %shard_map.51 = (bf16[2,448,4096]{2,1,0:T(8,128)(2,1)}, bf16[8,4096]{1,0:T(8,128)(2,1)}) custom-call(bf16[2,448,4096]{2,1,0:T(8,128)(2,1)S(1)} %get-tuple-element.6.final_ref, bf16[8,4096]{1,0:T(8,128)(2,1)S(1)} %get-tuple-element.7.router_ref), custom_call_target="tpu_custom_call" | custom-call | tf_op jit(solution)/shard_map/pallas_call | solution.py:340

commit v5 on v4

--- a/solution.py
+++ b/solution.py
@@ -47,7 +47,7 @@
         halves = [(0, nb // 2), (nb // 2, nb - nb // 2)] if na == 2 else [(0, nb)]
         first.append([Move(color, 0, ((a, 1), b, (0, nc))) for a in STEPS[na] for b in halves])
         second.append([Move(color, 1, (zero, (b, 1), (0, nc))) for b in STEPS[nb]])
-        third.append([Move(color, 1, ((1, na - 1), (b, 1), (0, nc))) for b in STEPS[nb]])
+        third.append([Move(color, 1, (a, (b, 1), (0, nc))) for a in ([(k, 1) for k in STEPS[na]] if nb == 2 else [(1, na - 1)]) for b in STEPS[nb]])
         early = [Move(color, 2, ((0, na), zero, (c, 1))) for c in STEPS[nc]]
         groups = [(b, 1) for b in STEPS[nb]] if nc == 2 else [(1, nb - 1)]
         late = [((0, na), b, (c, 1)) for c in STEPS[nc] for b in groups]
@@ -202,8 +202,7 @@
         ]
 
     starts = STAGES[0]
-    for m in starts[:HEAD]:
-        cast(m)
+    cast(starts[0])
     for c in small:
         c.wait()
     scaled = (weight[...] * gain[...]).astype(jnp.bfloat16).astype(jnp.float32)
@@ -211,6 +210,8 @@
         line % 2 == 0, jnp.broadcast_to(scaled[0:1, :], (8, width)), jnp.broadcast_to(scaled[1:2, :], (8, width))
     )
     parts[0] = pair.astype(jnp.bfloat16)
+    for m in starts[1:HEAD]:
+        cast(m)
     pl.semaphore_wait(barrier, len(peers) + OWNERS - 1)
     for k in range(1, OWNERS):
         part_copy(k).start()

time: 93.1 us -> 93.1 us (level)
  no operation moved by 1% of the time
where the time goes in v5:
time: 93.1 us; the launch traced here: 93 us
  Pallas kernels  92.4 us (99%)
    pallas_call x1, Pallas kernels, shards(): pl.pallas_call(functools.partial(kernel, cuts), out_shape=(pltpu.VMEM((ex...  89.3 us
    pallas_call x1, Pallas kernels, shards(): pl.pallas_call(drain, out_shape=(jax.ShapeDtypeStruct(final.shape, final....  3.12 us

profile of v5, /device:TPU:0, one launch (start us, length us, event | category | flops | bytes accessed | tf_op | source)
XLA Modules:
  0.0 93.0 jit_solution(2540831978142952292)
XLA Ops:
  0.6 89.3 %shard_map.50 = (bf16[2,448,4096]{2,1,0:T(8,128)(2,1)S(1)}, bf16[8,4096]{1,0:T(8,128)(2,1)S(1)}) custom-call(f32[2,14336,128]{2,1,0:T(8,128)} %x_ref.1, f32[2,128]{1,0:T(2,128)} %bitcast.4, f32[1,128]{1,0:T(1,128)} %bitcast.5), custom_call_target="tpu_custom_call" | custom-call | tf_op jit(solution)/shard_map/pallas_call | solution.py:313
  89.9 3.1 %shard_map.51 = (bf16[2,448,4096]{2,1,0:T(8,128)(2,1)}, bf16[8,4096]{1,0:T(8,128)(2,1)}) custom-call(bf16[2,448,4096]{2,1,0:T(8,128)(2,1)S(1)} %get-tuple-element.6.final_ref, bf16[8,4096]{1,0:T(8,128)(2,1)S(1)} %get-tuple-element.7.router_ref), custom_call_target="tpu_custom_call" | custom-call | tf_op jit(solution)/shard_map/pallas_call | solution.py:341

commit v6 on v4

--- a/solution.py
+++ b/solution.py
@@ -104,7 +104,7 @@
     for c in small:
         c.start()
     barrier = pltpu.get_barrier_semaphore()
-    for peer in peers.values():
+    for peer in [peers[d, SIZES[d] // 2] for d in (2, 1, 0)] + [peers[d, k] for d in (0, 1) for k in (1, 3)]:
         pl.semaphore_signal(barrier, inc=1, device_id=(own, peer), device_id_type=MESH)
     for k in range(1, OWNERS):
         pl.semaphore_signal(barrier, inc=1, device_id=(mates[k], me), device_id_type=MESH)
@@ -188,12 +188,12 @@
             device_id=(mates[k], me), device_id_type=MESH)
 
     def grid_copies(dim):
-        if dim == 0:
+        if dim == 2:
             block = grid.at[place[0], place[1], place[2]]
-        elif dim == 1:
-            block = grid.at[:, place[1], place[2]]
+        elif dim == 0:
+            block = grid.at[place[0], place[1]]
         else:
-            block = grid.at[:, :, place[2]]
+            block = grid.at[:, place[1]]
         return [
             pltpu.make_async_remote_copy(
                 src_ref=block, dst_ref=block, send_sem=grid_send.at[dim, k], recv_sem=grid_recv.at[dim, k],
@@ -248,7 +248,7 @@
                 tile = jnp.where(line // 2 == theirs, parts[j].astype(jnp.float32), tile)
             grid[place[0], place[1], place[2]] = tile.astype(jnp.bfloat16)
         if k == 1:
-            for c in grid_copies(0):
+            for c in grid_copies(2):
                 c.start()
     for m in STAGES[3]:
         for n in needs(m):
@@ -257,30 +257,29 @@
     for m in starts:
         await_arrival(m)
     settle()
+    for c in grid_copies(2):
+        c.wait()
     for c in grid_copies(0):
-        c.wait()
-    for c in grid_copies(1):
         c.start()
     for k, m in enumerate(STAGES[4]):
         for n in needs(m):
             await_arrival(n)
         copy(m).start()
         if k == 5:
+            for c in grid_copies(0):
+                c.wait()
             for c in grid_copies(1):
-                c.wait()
-            for c in grid_copies(2):
                 c.start()
     settle()
     for m in MOVES[: len(STAGES[0]) + len(STAGES[1]) + len(STAGES[2])]:
         copy(m).wait_send()
-    for c in grid_copies(2):
+    for c in grid_copies(1):
         c.wait()
     for row in range(32):
         router_ref[:, row * width : (row + 1) * width] = grid[row // 8, (row // 2) % 4, row % 2]
     for m in STAGES[3] + STAGES[4]:
         await_arrival(m)
         settle()
-    for m in STAGES[3] + STAGES[4]:
         copy(m).wait_send()
 
 

time: 93.1 us -> 93.3 us (level)
  no operation moved by 1% of the time
where the time goes in v6:
time: 93.3 us; the launch traced here: 93.2 us
  Pallas kernels  92.5 us (99%)
    pallas_call x1, Pallas kernels, shards(): pl.pallas_call(functools.partial(kernel, cuts), out_shape=(pltpu.VMEM((ex...  89.4 us
    pallas_call x1, Pallas kernels, shards(): pl.pallas_call(drain, out_shape=(jax.ShapeDtypeStruct(final.shape, final....  3.12 us

profile of v6, /device:TPU:0, one launch (start us, length us, event | category | flops | bytes accessed | tf_op | source)
XLA Modules:
  0.0 93.2 jit_solution(1516491085838507575)
XLA Ops:
  0.6 89.4 %shard_map.50 = (bf16[2,448,4096]{2,1,0:T(8,128)(2,1)S(1)}, bf16[8,4096]{1,0:T(8,128)(2,1)S(1)}) custom-call(f32[2,14336,128]{2,1,0:T(8,128)} %x_ref.1, f32[2,128]{1,0:T(2,128)} %bitcast.4, f32[1,128]{1,0:T(1,128)} %bitcast.5), custom_call_target="tpu_custom_call" | custom-call | tf_op jit(solution)/shard_map/pallas_call | solution.py:311
  90.1 3.1 %shard_map.51 = (bf16[2,448,4096]{2,1,0:T(8,128)(2,1)}, bf16[8,4096]{1,0:T(8,128)(2,1)}) custom-call(bf16[2,448,4096]{2,1,0:T(8,128)(2,1)S(1)} %get-tuple-element.6.final_ref, bf16[8,4096]{1,0:T(8,128)(2,1)S(1)} %get-tuple-element.7.router_ref), custom_call_target="tpu_custom_call" | custom-call | tf_op jit(solution)/shard_map/pallas_call | solution.py:339
